TPU v7x, 128 devices: a whole 4x4x4 slice. The times are simulated.
128 devices in a mesh: seq: 32 (over z_hi, x, y), head: 4 (over z_lo, core).
Axes of the slice: x: 4, y: 4, z: 4 (z_hi: 2, z_lo: 2; z = z_hi * 2 + z_lo), core: 2. Of those that a mesh axis runs over, the one named last changes fastest.
Arguments:
- latent: bfloat16 [4096, 1024], P('seq'), may hold values from -15 to 15
- probe: bfloat16 [4096, 1024], P('seq'), may hold values from -6 to 6
- time_embed: float32 [1024], replicated, may hold values from -6 to 6
- gain_attn: float32 [1024], replicated, may hold values from 0.1 to 1.9
- w_query: bfloat16 [1024, 1024], P(None, 'head'), may hold values from -0.625 to 0.625
- w_key: bfloat16 [1024, 1024], P(None, 'head'), may hold values from -11 to 11
- w_value: bfloat16 [1024, 1024], P(None, 'head'), may hold values from -0.1875 to 0.1875
- w_out: bfloat16 [1024, 1024], P('head'), may hold values from -0.1875 to 0.1875
- gain_mlp: float32 [1024], replicated, may hold values from 0.1 to 1.9
- w_in: bfloat16 [1024, 4096], P(None, 'head'), may hold values from -0.1875 to 0.1875
- w_down: bfloat16 [4096, 1024], P('head'), may hold values from -0.09375 to 0.09375
Outputs:
- latent_end: float32 [4096, 1024], P('seq')
- frame_trace: float32 [4096], P('seq')
- frame_logp: float32 [4096], P('seq')
- mean_logp: float32 [], replicated
All inputs are finite; a program needn't handle non-finite values.
Results may differ from a plain program's by a relative error of at most 0.03.
The roundings to bfloat16 on the way count: a program that leaves them out, or rounds other values in their place, can miss the bound.
Values may be sent and summed in bfloat16 or wider, within the bound.
A program may use at most 64 MiB of HBM per device.

v0:
```python
import math

import jax
import jax.numpy as jnp
from jax import lax
from jax.sharding import PartitionSpec as P

HEAD_DIM = 64
STEPS = 2


EPSILON = 1e-05
GELU_COEF = 0.044715
ROOT_TWO_PI = math.sqrt(2.0 / math.pi)


def side_by_side(arrays, axis, dim, along):
    both = jnp.concatenate(arrays, axis=along)
    filled, at, done = (lax.all_gather(both, axis, axis=dim, tiled=True), 0, [])
    for a in arrays:
        done.append(lax.slice_in_dim(filled, at, at + a.shape[along], axis=along))
        at += a.shape[along]
    return tuple(done)


def in_blocks(value, dim, devices):
    before, after = (value.shape[:dim], value.shape[dim + 1 :])
    return jnp.moveaxis(value.reshape(*before, devices, -1, *after), dim, 0)


def summed_on_arrival(value, axis, dim):
    tiles = in_blocks(value, dim, lax.axis_size(axis))
    arrived = lax.all_to_all(tiles, axis, split_axis=0, concat_axis=0, tiled=True)
    return arrived.sum(axis=0)


def sent_together(arrays, axis, dim, along):
    columns = [a.reshape(*a.shape[:along], -1) for a in arrays]
    both = jnp.concatenate(columns, axis=along)
    filled, at, done = (lax.all_gather(both, axis, axis=dim, tiled=True), 0, [])
    for a, column in zip(arrays, columns):
        piece = filled[..., at : at + column.shape[along]]
        done.append(piece.reshape(*piece.shape[:along], *a.shape[along:]))
        at += column.shape[along]
    return tuple(done)


def from_everyone(value, axis):
    copies = jnp.broadcast_to(value, (lax.axis_size(axis), *value.shape))
    return lax.all_to_all(copies, axis, split_axis=0, concat_axis=0, tiled=True)


def taken_together(value, axis):
    everything = from_everyone(value, axis)
    return jnp.sum(everything, axis=0)


def norm_pair(values, tangent, norm_gain):
    meansq = jnp.mean(values * values, axis=-1, keepdims=True) + EPSILON
    inverse = lax.rsqrt(meansq)
    inner_mean = jnp.mean(values * tangent, axis=-1, keepdims=True)
    primal = values * inverse * norm_gain
    derived = (tangent * inverse - values * inverse**3 * inner_mean) * norm_gain
    return (primal.astype(jnp.bfloat16), derived.astype(jnp.bfloat16))


def gelu_pair(pre_act, tangent):
    cubic_arg = pre_act + GELU_COEF * pre_act**3
    tanh_value = jnp.tanh(ROOT_TWO_PI * cubic_arg)
    output = 0.5 * pre_act * (1.0 + tanh_value)
    slope_value = 0.5 * (1.0 + tanh_value) + 0.5 * pre_act * (
        1.0 - tanh_value * tanh_value
    ) * ROOT_TWO_PI * (1.0 + 3.0 * GELU_COEF * pre_act * pre_act)
    return (output.astype(jnp.bfloat16), (slope_value * tangent).astype(jnp.bfloat16))


def split_heads(matrix):
    return matrix.reshape(matrix.shape[0], -1, HEAD_DIM)


def score_pair(queries, query_tang, keys, key_tang):
    scale = HEAD_DIM ** (-0.5)
    scores = jnp.einsum("rhd,shd->hrs", queries, keys, preferred_element_type=jnp.float32) * scale
    score_tang = (
        jnp.einsum("rhd,shd->hrs", query_tang, keys, preferred_element_type=jnp.float32)
        + jnp.einsum("rhd,shd->hrs", queries, key_tang, preferred_element_type=jnp.float32)
    ) * scale
    return (scores, score_tang)


def value_terms(rounded, rounded_tang, vals, val_tang):
    add_primal = jnp.einsum("hrs,shd->rhd", rounded, vals, preferred_element_type=jnp.float32)
    add_tang = jnp.einsum(
        "hrs,shd->rhd", rounded_tang, vals, preferred_element_type=jnp.float32
    ) + jnp.einsum("hrs,shd->rhd", rounded, val_tang, preferred_element_type=jnp.float32)
    return (add_primal, add_tang)


def attention(queries, query_tang, keys, vals, key_tang, val_tang):
    rows = queries.shape[0]
    local_cols = queries.shape[1]
    head_count = local_cols // HEAD_DIM
    query_heads = split_heads(queries)
    query_tang_heads = split_heads(query_tang)
    top_start = jnp.full((head_count, rows), -1e30, jnp.float32)
    piece = side_by_side((keys, vals, key_tang, val_tang), "seq", 0, 1)
    row_top = top_start
    keys_piece = split_heads(piece[0])
    vals_piece = split_heads(piece[1])
    key_tang_piece = split_heads(piece[2])
    val_tang_piece = split_heads(piece[3])
    scores, score_tang = score_pair(query_heads, query_tang_heads, keys_piece, key_tang_piece)
    new_top = jnp.maximum(row_top, jnp.max(scores, axis=-1))
    weights = jnp.exp(scores - new_top[:, :, None])
    weighted = weights * score_tang
    total = jnp.sum(weights, axis=-1)
    carried = jnp.sum(weighted, axis=-1)
    add_primal, add_tang = value_terms(
        weights.astype(jnp.bfloat16), weighted.astype(jnp.bfloat16), vals_piece, val_tang_piece
    )
    row_top, total, carried, acc_primal, acc_tang = (new_top, total, carried, add_primal, add_tang)
    total_t = jnp.transpose(total)[:, :, None]
    carried_t = jnp.transpose(carried)[:, :, None]
    primal = acc_primal / total_t
    tangent = acc_tang / total_t - carried_t / total_t * primal
    return (
        primal.reshape(rows, local_cols).astype(jnp.bfloat16),
        tangent.reshape(rows, local_cols).astype(jnp.bfloat16),
    )


def attend_rows(normed, normed_tang, w_query, w_key, w_value):
    rows = normed.shape[0]
    stacked = jnp.concatenate([normed, normed_tang], axis=0)

    def project(weight):
        both = jnp.dot(stacked, weight, preferred_element_type=jnp.float32).astype(jnp.bfloat16)
        return (both[:rows], both[rows:])

    queries, query_tang = project(w_query)
    keys, key_tang = project(w_key)
    vals, val_tang = project(w_value)
    return attention(queries, query_tang, keys, vals, key_tang, val_tang)


def hidden_pair(normed_mlp, normed_mlp_tang, w_in):
    rows = normed_mlp.shape[0]
    pre_both = jnp.dot(
        jnp.concatenate([normed_mlp, normed_mlp_tang], axis=0),
        w_in,
        preferred_element_type=jnp.float32,
    )
    return gelu_pair(pre_both[:rows], pre_both[rows:])


def pair_rows(first, second, weight, count):
    both = jnp.dot(
        jnp.concatenate([first, second], axis=0), weight, preferred_element_type=jnp.float32
    )
    return jnp.concatenate([both[:count], both[count:]], axis=1)


def gather_rows(first, second):
    return side_by_side((first, second), "head", 0, 1)


def share_field(
    inputs, direction, gain_attn, w_query, w_key, w_value, w_out, gain_mlp, w_in, w_down
):
    share = inputs.shape[0]
    width = inputs.shape[1]
    normed, normed_tang = norm_pair(inputs, direction, gain_attn)
    normed, normed_tang = gather_rows(normed, normed_tang)
    head_out, head_tang = attend_rows(normed, normed_tang, w_query, w_key, w_value)
    attn_both = summed_on_arrival(
        pair_rows(head_out, head_tang, w_out, share * lax.axis_size("head")), "head", 0
    )
    attn = attn_both[:, :width]
    attn_tang = attn_both[:, width:]
    middle = inputs + attn
    middle_tang = direction + attn_tang
    normed_mlp, normed_mlp_tang = norm_pair(middle, middle_tang, gain_mlp)
    normed_mlp, normed_mlp_tang = gather_rows(normed_mlp, normed_mlp_tang)
    activ, activ_tang = hidden_pair(normed_mlp, normed_mlp_tang, w_in)
    mlp_both = summed_on_arrival(
        pair_rows(activ, activ_tang, w_down, share * lax.axis_size("head")), "head", 0
    )
    return (attn + mlp_both[:, :width], attn_tang + mlp_both[:, width:])


def per_device(
    latent, probe, time_embed, gain_attn, w_query, w_key, w_value, w_out, gain_mlp, w_in, w_down
):
    rows = latent.shape[0]
    width = latent.shape[1]
    share = rows // lax.axis_size("head")
    offset = lax.axis_index("head") * share
    state = lax.dynamic_slice_in_dim(latent, offset, share, 0).astype(jnp.float32)
    direction = lax.dynamic_slice_in_dim(probe, offset, share, 0).astype(jnp.float32)
    trace = jnp.zeros((share,), jnp.float32)
    for euler_step in range(STEPS):
        inputs = state + euler_step / STEPS * time_embed
        field, field_tang = share_field(
            inputs, direction, gain_attn, w_query, w_key, w_value, w_out, gain_mlp, w_in, w_down
        )
        trace = trace + jnp.sum(direction * field_tang, axis=-1) / (STEPS * width)
        state = state + field / STEPS
    state, trace = sent_together((state, trace), "head", 0, 1)
    frame_logp = (
        trace - 0.5 * jnp.sum(state * state, axis=-1) / width - 0.5 * math.log(2.0 * math.pi)
    )
    grand_total = taken_together(jnp.sum(frame_logp), "seq")
    mean_logp = grand_total / (rows * lax.axis_size("seq"))
    return (state, trace, frame_logp, mean_logp)


def solution(mesh):
    return jax.shard_map(
        per_device,
        mesh=mesh,
        in_specs=(
            P("seq", None),
            P("seq", None),
            P(),
            P(),
            P(None, "head"),
            P(None, "head"),
            P(None, "head"),
            P("head", None),
            P(),
            P(None, "head"),
            P("head", None),
        ),
        out_specs=(P("seq", None), P("seq"), P("seq"), P()),
        check_vma=False,
    )
```

profile of v0, /device:TPU:0, one launch (start us, length us, event | category | flops | bytes accessed | tf_op | source)
XLA Modules:
  0.0 489.4 jit_solution(6684413240899564756)
XLA Ops:
  10.2 7.7 %all_gather.21 = bf16[128,2048]{1,0:T(8,128)(2,1)S(1)} all-gather(bf16[32,2048]{1,0:T(8,128)(2,1)S(1)} %pad_maximum_fusion.15), channel_id=1, replica_groups=mesh['seq'=32,'head'=4] {'head'}, dimensions={0}, use_global_device_ids=true | all-gather | bytes 655360 | tf_op jit(solution)/shard_map/all_gather | solution.py:19
  17.9 1.4 convolution_convert_fusion.4
  19.3 1.4 convolution_convert_fusion.5
  21.9 142.5 %all-gather.3.cloned.1.call-done = bf16[4096,1024]{0,1:T(8,128)(2,1)} async-done(((bf16[128,1024]{0,1:T(8,128)(2,1)}), bf16[4096,1024]{0,1:T(8,128)(2,1)}) %all-gather.3.cloned.1.call-update) | async-done | bytes 8388624 | tf_op jit(solution)/shard_map/all_gather | solution.py:19
  164.4 4.8 fusion.127
  169.2 1.4 multiply_reduce_fusion.1
  170.6 1.5 fusion
  172.1 1.7 fusion.43
  175.1 4.7 fusion.142
  179.8 1.7 fusion.143
  182.0 1.6 fusion.37
  184.1 17.6 %all_to_all.26 = f32[4,32,2048]{2,1,0:T(8,128)} all-to-all(f32[4,32,2048]{2,1,0:T(8,128)S(1)} %bitcast.98), channel_id=1, replica_groups=mesh['seq'=32,'head'=4] {'head'}, dimensions={0} | all-to-all | bytes 2097152 | tf_op jit(solution)/shard_map/all_to_all | solution.py:33
  201.7 1.3 reduce_sum.193
  203.4 6.6 %all_gather.23 = bf16[128,2048]{1,0:T(8,128)(2,1)S(1)} all-gather(bf16[32,2048]{1,0:T(8,128)(2,1)S(1)} %pad_maximum_fusion.16), channel_id=1, replica_groups=mesh['seq'=32,'head'=4] {'head'}, dimensions={0}, use_global_device_ids=true | all-gather | bytes 655360 | tf_op jit(solution)/shard_map/all_gather | solution.py:19
  212.1 17.6 %all_to_all.27 = f32[4,32,2048]{2,1,0:T(8,128)} all-to-all(f32[4,32,2048]{2,1,0:T(8,128)S(1)} %bitcast.99), channel_id=1, replica_groups=mesh['seq'=32,'head'=4] {'head'}, dimensions={0} | all-to-all | bytes 2097152 | tf_op jit(solution)/shard_map/all_to_all | solution.py:33
  229.7 2.0 reduce_sum.196
  233.0 6.5 %all_gather.24 = bf16[128,2048]{1,0:T(8,128)(2,1)S(1)} all-gather(bf16[32,2048]{1,0:T(8,128)(2,1)S(1)} %pad_maximum_fusion.17), channel_id=1, replica_groups=mesh['seq'=32,'head'=4] {'head'}, dimensions={0}, use_global_device_ids=true | all-gather | bytes 655360 | tf_op jit(solution)/shard_map/all_gather | solution.py:19
  239.5 1.5 convolution_convert_fusion.1
  242.2 1.5 convolution_convert_fusion
  244.3 137.6 %all-gather.5.cloned.1.call-done = bf16[4096,1024]{0,1:T(8,128)(2,1)} async-done(((bf16[128,1024]{0,1:T(8,128)(2,1)}), bf16[4096,1024]{0,1:T(8,128)(2,1)}) %all-gather.5.cloned.1.call-update) | async-done | bytes 8388624 | tf_op jit(solution)/shard_map/all_gather | solution.py:19
  381.9 4.8 fusion.126
  386.7 1.4 multiply_reduce_fusion
  388.1 2.1 fusion.2
  390.2 1.7 fusion.40
  393.2 6.1 %fusion.144 = (f32[4,128]{1,0:T(4,128)}, bf16[4,128,4096]{2,1,0:T(8,128)(2,1)}) fusion(f32[4,128,4096]{2,1,0:T(8,128)S(1)} %fusion.147, bf16[128,4,64]{0,2,1:T(8,128)(2,1)S(1)} %bitcast.105, bf16[4096,4,64]{0,2,1:T(8,128)(2,1)S(1)} %bitcast.95, f32[4,128]{1,0:T(4,128)} %copy-done.12, f32[4,128,4096]{2,1,0:T(8,128)S(1)} %get-tuple-element.86), kind=kOutput, calls=%fused_computation.201 | convolution fusion | flops 283115008 | bytes 23138304 | tf_op jit(solution)/shard_map/rhd,shd->hrs/dot_general | solution.py:86
  400.0 2.5 fusion.145
  402.5 1.6 fusion.34
  404.6 17.6 %all_to_all.28 = f32[4,32,2048]{2,1,0:T(8,128)} all-to-all(f32[4,32,2048]{2,1,0:T(8,128)S(1)} %bitcast.100), channel_id=1, replica_groups=mesh['seq'=32,'head'=4] {'head'}, dimensions={0} | all-to-all | bytes 2097152 | tf_op jit(solution)/shard_map/all_to_all | solution.py:33
  425.7 6.7 %all_gather.26 = bf16[128,2048]{1,0:T(8,128)(2,1)S(1)} all-gather(bf16[32,2048]{1,0:T(8,128)(2,1)S(1)} %pad_maximum_fusion.18), channel_id=1, replica_groups=mesh['seq'=32,'head'=4] {'head'}, dimensions={0}, use_global_device_ids=true | all-gather | bytes 655360 | tf_op jit(solution)/shard_map/all_gather | solution.py:19
  434.4 17.6 %all_to_all.29 = f32[4,32,2048]{2,1,0:T(8,128)} all-to-all(f32[4,32,2048]{2,1,0:T(8,128)S(1)} %bitcast.101), channel_id=1, replica_groups=mesh['seq'=32,'head'=4] {'head'}, dimensions={0} | all-to-all | bytes 2097152 | tf_op jit(solution)/shard_map/all_to_all | solution.py:33
  454.6 6.8 %all_gather.27 = f32[128,1025]{1,0:T(8,128)S(1)} all-gather(f32[32,1025]{1,0:T(8,128)S(1)} %pad_maximum_fusion.14), channel_id=1, replica_groups=mesh['seq'=32,'head'=4] {'head'}, dimensions={0}, use_global_device_ids=true | all-gather | bytes 656000 | tf_op jit(solution)/shard_map/all_gather | solution.py:40
  464.1 16.1 %all_to_all.30 = f32[32,1,1]{2,1,0:T(1,128)S(1)} all-to-all(f32[32,1,1]{2,1,0:T(1,128)S(1)} %broadcast_in_dim.2), channel_id=1, replica_groups=mesh['seq'=32,'head'=4] {'seq'}, dimensions={0} | all-to-all | bytes 256 | tf_op jit(solution)/shard_map/all_to_all | solution.py:50
  (111 shorter events, 25.7 us)
Async XLA Ops:
  7.2 202.9 %copy-start = (bf16[1024,1024]{1,0:T(8,128)(2,1)S(1)}, bf16[1024,1024]{1,0:T(8,128)(2,1)}, u32[]{:S(2)}) copy-start(bf16[1024,1024]{1,0:T(8,128)(2,1)} %param.20) | copy-start | bytes 6291460
  7.2 14.3 %copy-start.19 = (bf16[1024,256]{1,0:T(8,128)(2,1)S(1)}, bf16[1024,256]{1,0:T(8,128)(2,1)}, u32[]{:S(2)}) copy-start(bf16[1024,256]{1,0:T(8,128)(2,1)} %param.15) | copy-start | bytes 1572868
  7.2 157.2 %all-gather.3.cloned.1.call-start = ((), (), s32[]{:S(2)}) async-start(), calls=%async_computation.5 | async-start | bytes 8650752 | tf_op jit(solution)/shard_map/all_gather | solution.py:19
  21.5 360.4 %all-gather.5.cloned.1.call-start = ((), (), s32[]{:S(2)}) async-start(), calls=%async_computation.6 | async-start | bytes 8650752 | tf_op jit(solution)/shard_map/all_gather | solution.py:19
  175.1 4.7 copy-start.1
  179.8 2.2 copy-start.3
  181.5 2.1 copy-start.7
  183.9 19.1 %copy-start.8 = (bf16[128,1024]{1,0:T(8,128)(2,1)S(1)}, bf16[128,1024]{1,0:T(8,128)(2,1)}, u32[]{:S(2)}) copy-start(bf16[128,1024]{1,0:T(8,128)(2,1)} %param.12) | copy-start | bytes 786436
  183.9 19.1 %copy-start.10 = (bf16[128,1024]{1,0:T(8,128)(2,1)S(1)}, bf16[128,1024]{1,0:T(8,128)(2,1)}, u32[]{:S(2)}) copy-start(bf16[128,1024]{1,0:T(8,128)(2,1)} %param.11) | copy-start | bytes 786436
  184.0 19.3 %copy-start.15 = (f32[1024]{0:T(1024)S(1)}, f32[1024]{0:T(1024)}, u32[]{:S(2)}) copy-start(f32[1024]{0:T(1024)} %param.19) | copy-start | bytes 12292
  203.0 8.1 %copy-start.5 = (bf16[1024,1024]{1,0:T(8,128)(2,1)S(1)}, bf16[1024,1024]{1,0:T(8,128)(2,1)}, u32[]{:S(2)}) copy-start(bf16[1024,1024]{1,0:T(8,128)(2,1)} %param.21) | copy-start | bytes 6291460
  211.9 20.9 %copy-start.14 = (f32[1024]{0:T(1024)S(1)}, f32[1024]{0:T(1024)}, u32[]{:S(2)}) copy-start(f32[1024]{0:T(1024)} %param.14) | copy-start | bytes 12292
  231.7 9.4 %copy-start.18 = (bf16[1024,256]{1,0:T(8,128)(2,1)S(1)}, bf16[1024,256]{1,0:T(8,128)(2,1)}, u32[]{:S(2)}) copy-start(bf16[1024,256]{1,0:T(8,128)(2,1)} %param.16) | copy-start | bytes 1572868
  239.5 1.5 copy-start.11
  388.1 2.1 copy-start.12
  390.2 1.7 copy-start.9
  393.2 6.8 %copy-start.2 = (bf16[4096,256]{0,1:T(8,128)(2,1)S(1)}, bf16[4096,256]{0,1:T(8,128)(2,1)}, u32[]{:S(2)}) copy-start(bf16[4096,256]{0,1:T(8,128)(2,1)} %get-tuple-element.23) | copy-start | bytes 6291460
  400.0 2.5 copy-start.4
  400.0 2.5 copy-start.13
  404.4 20.2 %copy-start.16 = (f32[1024]{0:T(1024)S(1)}, f32[1024]{0:T(1024)}, u32[]{:S(2)}) copy-start(f32[1024]{0:T(1024)} %param.19) | copy-start | bytes 12292
  423.5 10.0 %copy-start.6 = (bf16[1024,1024]{1,0:T(8,128)(2,1)S(1)}, bf16[1024,1024]{1,0:T(8,128)(2,1)}, u32[]{:S(2)}) copy-start(bf16[1024,1024]{1,0:T(8,128)(2,1)} %param.21) | copy-start | bytes 6291460
  462.3 19.2 %copy-start.17 = (f32[128]{0:T(128)}, f32[128]{0:T(128)S(1)}, u32[]{:S(2)}) copy-start(f32[128]{0:T(128)S(1)} %slice_reduce_fusion) | copy-start | bytes 1540
Sparse Core Ops, SparseCore 0:
  21.6 142.7 all-gather.2
  242.3 139.5 all-gather.4
where the time goes:
time: 490 us; the launch traced here: 489 us
  waiting for transfers between devices  280 us (57%)
  blocking collectives  121 us (25%)
  matrix products  36.7 us (7%)
  other arithmetic  23.1 us (5%)
  between operations  16.4 us (3%)
  local copies, waits for them, and re-layouts  12.3 us (3%)
    all_gather x2, waiting for transfers between devices, side_by_side(): filled, at, done = (lax.all_gather(both, axis, axis=dim, tiled=True), 0, [])  280 us
    all_to_all x4, blocking collectives, summed_on_arrival(): lax.all_to_all(tiles, axis, split_axis=0, concat_axis=0, tiled=True)  70.3 us
    all_gather x4, blocking collectives, side_by_side(): filled, at, done = (lax.all_gather(both, axis, axis=dim, tiled=True), 0, [])  27.6 us
    all_to_all x1, blocking collectives, from_everyone(): return lax.all_to_all(copies, axis, split_axis=0, concat_axis=0, tiled=True)  16.1 us
    dot_general x2, matrix products, score_pair(): jnp.einsum('rhd,shd->hrs', queries, key_tang, preferred_element_type=jnp....  10.8 us
  transfers between devices with their start and end apart: 2, of which 2 were waited for; matrix products, arithmetic and copies ran while one was open for 1% of the time, Pallas kernels for 0%

commit v1 on v0

v1 whole, which is shorter than its diff:
```python
import functools
import math

import jax
import jax.numpy as jnp
from jax import lax
from jax.experimental import pallas as pl
from jax.experimental.pallas import tpu as pltpu
from jax.sharding import PartitionSpec as P

HEAD_DIM = 64
STEPS = 2
EPSILON = 1e-05
GELU_COEF = 0.044715
ROOT_TWO_PI = math.sqrt(2.0 / math.pi)

ROWS = 64
SEQ_ROWS = 128
WIDTH = 1024
RING = 4
QROWS = 512
NEG = -1e30

OWN, LEFT, RIGHT, FAR, ZOWN, ZLEFT, ZRIGHT, ZFAR = range(8)

f32 = jnp.float32
bf16 = jnp.bfloat16


def norm_pair(values, tangent, norm_gain):
    meansq = jnp.mean(values * values, axis=-1, keepdims=True) + EPSILON
    inverse = lax.rsqrt(meansq)
    inner_mean = jnp.mean(values * tangent, axis=-1, keepdims=True)
    primal = values * inverse * norm_gain
    derived = (tangent * inverse - values * inverse**3 * inner_mean) * norm_gain
    return jnp.concatenate([primal.astype(bf16), derived.astype(bf16)], axis=0)


def gelu_pair(pre_act, tangent):
    cubic_arg = pre_act + GELU_COEF * pre_act * pre_act * pre_act
    tanh_value = jnp.tanh(ROOT_TWO_PI * cubic_arg)
    output = 0.5 * pre_act * (1.0 + tanh_value)
    slope_value = 0.5 * (1.0 + tanh_value) + 0.5 * pre_act * (
        1.0 - tanh_value * tanh_value
    ) * ROOT_TWO_PI * (1.0 + 3.0 * GELU_COEF * pre_act * pre_act)
    return (output.astype(bf16), (slope_value * tangent).astype(bf16))


def swap_halves(tile):
    return pltpu.roll(tile, HEAD_DIM, 1)


def kernel(
    latent, probe, time_embed, gain_attn, w_query, w_key, w_value, w_out, gain_mlp, w_in, w_down,
    o_state, o_trace, o_logp, o_mean,
    lat_in, prb_in, wq, wk, wv, wo, wi, wd,
    state, direction, inputs_s, trace_s, attn_s, normed_s, act_s,
    stage_kv, stage_q, kv, qin, q1, q2, relay, acc_p, acc_t, top_s, total_s, carried_s,
    ret_stage, ret, red_send, red_recv, stat_mine, stat_in, mean_send, mean_recv,
    load_sem, wsend, wrecv, kv_send, kv_recv, q_send, q_recv, self_sem, g_send, g_recv, r_recv,
    ret_send, ret_recv, red_ssem, red_rsem, fin_send, fin_recv, mean_ssem, mean_rsem,
):
    s = lax.axis_index("seq")
    hd = lax.axis_index("head")
    x = lax.rem(s // 4, 4)
    y = lax.rem(s, 4)
    c = lax.rem(hd, 2)
    other = 1 - c
    zlo = hd // 2
    z = (s // 16) * 2 + zlo
    a = y + c * (x - y)
    g = x + c * (y - x)

    def place(aa, gg, zz, cc):
        aa, gg, zz = lax.rem(aa, 4), lax.rem(gg, 4), lax.rem(zz, 4)
        xx = gg + c * (aa - gg)
        yy = aa + c * (gg - aa)
        return ((zz // 2) * 16 + xx * 4 + yy, lax.rem(zz, 2) * 2 + cc)

    def remote(src, dst, ssem, rsem, where):
        return pltpu.make_async_remote_copy(
            src_ref=src, dst_ref=dst, send_sem=ssem, recv_sem=rsem,
            device_id=where, device_id_type=pl.DeviceIdType.MESH,
        )

    here = place(a, g, z, other)
    zn = z + 1 + 2 * c
    zpair = z + 1 - 2 * zlo

    barrier = pltpu.get_barrier_semaphore()
    greeted = (
        [place(a + d, g, z, c) for d in (1, 2, 3)]
        + [place(a + d, g, z, other) for d in range(4)]
        + [place(a, g + d, z, other) for d in (1, 2, 3)]
        + [place(a, g + d, z, c) for d in (1, 2, 3)]
        + [place(a, g, z + d, c) for d in (1, 2, 3)]
    )
    for where in greeted:
        pl.semaphore_signal(
            barrier, inc=1, device_id=where, device_id_type=pl.DeviceIdType.MESH
        )

    row0 = pl.multiple_of(c * ROWS, ROWS)
    loads = [
        pltpu.make_async_copy(latent.at[pl.ds(row0, ROWS)], lat_in, load_sem.at[0]),
        pltpu.make_async_copy(probe.at[pl.ds(row0, ROWS)], prb_in, load_sem.at[1]),
    ]
    weights = [(w_query, wq), (w_key, wk), (w_value, wv), (w_out, wo), (w_in, wi), (w_down, wd)]
    for i, (src, dst) in enumerate(weights):
        loads.append(pltpu.make_async_copy(src, dst.at[c], load_sem.at[2 + i]))
    for load in loads:
        load.start()
    pl.semaphore_wait(barrier, len(greeted))
    swaps = [
        remote(src, dst.at[c], wsend.at[i], wrecv.at[i], here)
        for i, (src, dst) in enumerate(weights)
    ]
    for swap in swaps:
        swap.start()

    loads[0].wait()
    loads[1].wait()
    state[...] = lat_in[...].astype(f32)
    direction[...] = prb_in[...].astype(f32)
    trace_s[...] = jnp.zeros_like(trace_s)

    lane = lax.broadcasted_iota(jnp.int32, (ROWS, 128), 1)
    low = lane < HEAD_DIM
    low_c = lax.broadcasted_iota(jnp.int32, (128, 128), 1) < HEAD_DIM

    def weights_here(i):
        loads[2 + i].wait()
        swaps[i].wait()

    for i in range(6):
        weights_here(i)

    def one_step(t, carry):
        inputs = state[...] + (t.astype(f32) / STEPS) * time_embed[...]
        inputs_s[...] = inputs
        normed_s[...] = norm_pair(inputs, direction[...], gain_attn[...])
        normed = normed_s[...]

        for cc in range(2):
            for which, weight in enumerate((wk, wv, wq)):
                both = jnp.dot(normed, weight[cc], preferred_element_type=f32)
                if which == 2:
                    both = both * (HEAD_DIM**-0.5)
                for j in range(2):
                    prim = both[:ROWS, j * 128 : (j + 1) * 128]
                    tang = both[ROWS:, j * 128 : (j + 1) * 128]
                    first = jnp.where(low, prim, swap_halves(tang)).astype(bf16)
                    second = jnp.where(low, swap_halves(prim), tang).astype(bf16)
                    if which == 2:
                        stage_q[t, cc, 2 * j] = first
                        stage_q[t, cc, 2 * j + 1] = second
                    else:
                        stage_kv[t, cc, 2 * j, :, which * 128 : (which + 1) * 128] = first
                        stage_kv[t, cc, 2 * j + 1, :, which * 128 : (which + 1) * 128] = second

        def kv_slot(slot, kind):
            return kv.at[t, OWN, pl.ds((slot * 2 + kind) * ROWS, ROWS)]

        def q_slot(slot, kind):
            return qin.at[t, slot * 2 + kind]

        kv_out, q_out = [], []
        for d in (0, 1, 3, 2):
            slot = (4 - d) % 4
            for kind in (1, 0):
                if kind == 0 and d == 0:
                    continue
                if kind == 0:
                    cc, to, head = c, place(a + d, g, z, c), lax.rem(a + d, 4)
                else:
                    cc, to, head = other, place(a, g + d, z, other), lax.rem(g + d, 4)
                n = slot * 2 + kind
                kv_out.append(remote(
                    stage_kv.at[t, cc, head], kv_slot(slot, kind),
                    kv_send.at[t, n], kv_recv.at[t, n], to,
                ))
                q_out.append(remote(
                    stage_q.at[t, cc, head], q_slot(slot, kind),
                    q_send.at[t, n], q_recv.at[t, n], to,
                ))
        for copy in kv_out:
            copy.start()
        for copy in q_out:
            copy.start()
        kv_self = pltpu.make_async_copy(stage_kv.at[t, c, a], kv_slot(0, 0), self_sem.at[0])
        q_self = pltpu.make_async_copy(stage_q.at[t, c, a], q_slot(0, 0), self_sem.at[1])
        kv_self.start()
        q_self.start()

        def piece(block, p):
            return kv.at[t, block, pl.ds(p * 128, 128)]

        sent = []

        def send(src, block, p, to):
            n = len(sent)
            copy = remote(src, piece(block, p), g_send.at[t, n], g_recv.at[t, block, p], to)
            copy.start()
            sent.append(copy)

        right, left = place(a, g + 1, z, c), place(a, g + 3, z, c)
        onward = place(a, g, zn, c)

        def arrived(block, p):
            remote(
                piece(block, p), piece(block, p), g_send.at[t, 0], g_recv.at[t, block, p], right
            ).wait_recv()

        for slot in (0, 1, 3, 2):
            for kind in range(2):
                if slot == 0 and kind == 0:
                    kv_self.wait()
                else:
                    n = slot * 2 + kind
                    remote(
                        kv_slot(slot, kind), kv_slot(slot, kind), kv_send.at[t, n],
                        kv_recv.at[t, n], right,
                    ).wait_recv()
            send(piece(OWN, slot), LEFT, slot, right)
            send(piece(OWN, slot), RIGHT, slot, left)
            n = len(sent)
            copy = remote(
                piece(OWN, slot), relay.at[t, pl.ds(slot * 128, 128)], g_send.at[t, n],
                r_recv.at[t, slot], onward,
            )
            copy.start()
            sent.append(copy)

        for n in range(8):
            if n == 0:
                q_self.wait()
            else:
                remote(
                    qin.at[t, n], qin.at[t, n], q_send.at[t, n], q_recv.at[t, n], right
                ).wait_recv()

        def prepare(n, carry):
            tile = qin[t, n].astype(f32)
            q1[pl.ds(n * ROWS, ROWS), :] = jnp.where(low, tile, 0.0).astype(bf16)
            q2[pl.ds(n * ROWS, ROWS), :] = swap_halves(tile).astype(bf16)
            return carry

        lax.fori_loop(0, 8, prepare, 0)
        acc_p[...] = jnp.zeros_like(acc_p)
        acc_t[...] = jnp.zeros_like(acc_t)
        total_s[...] = jnp.zeros_like(total_s)
        carried_s[...] = jnp.zeros_like(carried_s)
        top_s[...] = jnp.full_like(top_s, NEG)

        def attend(block):
            keys = kv[t, block, :, 0:128]
            vals = kv[t, block, :, 128:256]
            nt = (((1,), (1,)), ((), ()))

            def chunk(i, carry):
                at = pl.ds(pl.multiple_of(i * 128, 128), 128)
                scores = lax.dot_general(q1[at, :], keys, nt, preferred_element_type=f32)
                tangs = lax.dot_general(q2[at, :], keys, nt, preferred_element_type=f32)
                old = top_s[at, :]
                new = jnp.maximum(old, jnp.max(scores, axis=-1, keepdims=True))
                fade = jnp.exp(old - new)
                top_s[at, :] = new
                weights_ = jnp.exp(scores - jnp.concatenate([new] * 4, axis=1))
                weighted = weights_ * tangs
                tot = fade * total_s[at, :]
                car = fade * carried_s[at, :]
                for k in range(4):
                    tot = tot + weights_[:, k * 128 : (k + 1) * 128]
                    car = car + weighted[:, k * 128 : (k + 1) * 128]
                total_s[at, :] = tot
                carried_s[at, :] = car
                acc_p[at, :] = fade * acc_p[at, :] + jnp.dot(
                    weights_.astype(bf16), vals, preferred_element_type=f32
                )
                acc_t[at, :] = fade * acc_t[at, :] + jnp.dot(
                    weighted.astype(bf16), vals, preferred_element_type=f32
                )
                return carry

            lax.fori_loop(0, 4, chunk, 0, unroll=True)

        attend(OWN)
        for p in (0, 1, 3, 2):
            part = relay.at[t, pl.ds(p * 128, 128)]
            remote(part, part, g_send.at[t, 0], r_recv.at[t, p], right).wait_recv()
            send(part, ZOWN, p, onward)
        for p in (0, 1):
            arrived(LEFT, p)
            send(piece(LEFT, p), FAR, p, right)
        for p in (3, 2):
            arrived(RIGHT, p)
            send(piece(RIGHT, p), FAR, p, left)
        arrived(LEFT, 3)
        arrived(LEFT, 2)
        attend(LEFT)
        arrived(RIGHT, 0)
        arrived(RIGHT, 1)
        attend(RIGHT)
        for p in (0, 1, 3, 2):
            arrived(ZOWN, p)
            send(piece(ZOWN, p), ZLEFT, p, right)
            send(piece(ZOWN, p), ZRIGHT, p, left)
        attend(ZOWN)
        for p in range(4):
            arrived(FAR, p)
        attend(FAR)
        for p in (0, 1):
            arrived(ZLEFT, p)
            send(piece(ZLEFT, p), ZFAR, p, right)
        for p in (3, 2):
            arrived(ZRIGHT, p)
            send(piece(ZRIGHT, p), ZFAR, p, left)
        arrived(ZLEFT, 3)
        arrived(ZLEFT, 2)
        attend(ZLEFT)
        arrived(ZRIGHT, 0)
        arrived(ZRIGHT, 1)
        attend(ZRIGHT)
        for p in range(4):
            arrived(ZFAR, p)
        attend(ZFAR)

        def finish(i, carry):
            at = pl.ds(pl.multiple_of(i * 128, 128), 128)
            total = jnp.sum(total_s[at, :], axis=-1, keepdims=True)
            carried = jnp.sum(carried_s[at, :], axis=-1, keepdims=True)
            ap = acc_p[at, :]
            prim = ap / total
            tang = (acc_t[at, :] + swap_halves(ap)) / total - (carried / total) * prim
            out = jnp.where(low_c, prim, swap_halves(tang)).astype(bf16)
            ret_stage[t, 2 * i] = out[:ROWS]
            ret_stage[t, 2 * i + 1] = out[ROWS:]
            return carry

        lax.fori_loop(0, 4, finish, 0)

        back = []
        for slot in (2, 1, 3, 0):
            for kind in (0, 1):
                n = slot * 2 + kind
                if n == 0:
                    continue
                m = ((4 - slot) % 4) * 2 + kind
                to = place(a + slot, g, z, c if kind == 0 else other)
                copy = remote(
                    ret_stage.at[t, n], ret.at[t, c, a], ret_send.at[t, n], ret_recv.at[t, m], to
                )
                copy.start()
                back.append(copy)
        ret_self = pltpu.make_async_copy(ret_stage.at[t, 0], ret.at[t, c, a], self_sem.at[2])
        ret_self.start()
        ret_self.wait()
        for m in range(1, 8):
            remote(
                ret_stage.at[t, 0], ret.at[t, 0, 0], ret_send.at[t, m], ret_recv.at[t, m], right
            ).wait_recv()

        def reduced_start(phase, at, value):
            red_send[t, phase, :, at] = value.astype(bf16)

        def reduce_copy(phase):
            return remote(
                red_send.at[t, phase], red_recv.at[t, phase], red_ssem.at[t, phase],
                red_rsem.at[t, phase], place(a, g, zpair, c),
            )

        def reduced(phase):
            return red_send[t, phase].astype(f32) + red_recv[t, phase].astype(f32)

        prims, tangs = [], []
        for cc in range(2):
            for j in range(2):
                first = ret[t, cc, 2 * j].astype(f32)
                second = ret[t, cc, 2 * j + 1].astype(f32)
                prims.append(jnp.where(low, first, swap_halves(second)).astype(bf16))
                tangs.append(jnp.where(low, swap_halves(first), second).astype(bf16))
        part = jnp.zeros((2 * ROWS, WIDTH), f32)
        for cc in range(2):
            heads = jnp.concatenate(
                [
                    jnp.concatenate(prims[2 * cc : 2 * cc + 2], axis=1),
                    jnp.concatenate(tangs[2 * cc : 2 * cc + 2], axis=1),
                ],
                axis=0,
            )
            part = part + jnp.dot(heads, wo[cc], preferred_element_type=f32)
        red_send[t, 0] = part.astype(bf16)
        first_sum = reduce_copy(0)
        first_sum.start()
        first_sum.wait()
        attn_s[...] = reduced(0)
        middle = inputs_s[...] + attn_s[:ROWS, :]
        middle_tang = direction[...] + attn_s[ROWS:, :]
        normed_s[...] = norm_pair(middle, middle_tang, gain_mlp[...])

        normed2 = normed_s[...]
        for cc in range(2):
            def hidden(j, carry):
                at = pl.ds(pl.multiple_of(j * 256, 256), 256)
                pre = jnp.dot(normed2, wi[cc, :, at], preferred_element_type=f32)
                act, act_tang = gelu_pair(pre[:ROWS], pre[ROWS:])
                act_s[cc, :ROWS, at] = act
                act_s[cc, ROWS:, at] = act_tang
                return carry

            lax.fori_loop(0, 4, hidden, 0)
        for j in range(4):
            at = slice(j * 256, (j + 1) * 256)
            red_send[t, 1, :, at] = (
                jnp.dot(act_s[0], wd[0, :, at], preferred_element_type=f32)
                + jnp.dot(act_s[1], wd[1, :, at], preferred_element_type=f32)
            ).astype(bf16)
        second_sum = reduce_copy(1)
        second_sum.start()
        second_sum.wait()
        field = attn_s[...] + reduced(1)
        trace_s[...] = trace_s[...] + jnp.sum(
            direction[...] * field[ROWS:], axis=-1, keepdims=True
        ) / (STEPS * WIDTH)
        state[...] = state[...] + field[:ROWS] / STEPS

        for copy in kv_out + q_out + sent + back:
            copy.wait_send()
        return carry

    lax.fori_loop(0, STEPS, one_step, 0)

    final = state[...]
    trace = trace_s[...]
    logp = (
        trace
        - 0.5 * jnp.sum(final * final, axis=-1, keepdims=True) / WIDTH
        - 0.5 * math.log(2.0 * math.pi)
    )
    stat_mine[0] = trace
    stat_mine[1] = logp
    spot = lax.broadcasted_iota(jnp.int32, (8, 128), 1) == s * 2 + c
    mean_send[0] = jnp.where(spot, jnp.sum(logp, axis=0, keepdims=True), 0.0)
    mine = pl.ds(row0, ROWS)
    finals = [
        remote(state, o_state.at[mine], fin_send.at[0], fin_recv.at[0], here),
        remote(stat_mine, stat_in, fin_send.at[1], fin_recv.at[1], here),
    ]
    for copy in finals:
        copy.start()
    o_state[mine, :] = final

    copies = []
    for d in range(4):
        slot = (4 - d) % 4
        for kind in range(2):
            if kind == 0 and d == 0:
                continue
            to = place(a + d, g, z, c) if kind == 0 else place(a, g + d, z, other)
            n = slot * 2 + kind
            copies.append(remote(
                mean_send.at[0], mean_recv.at[n], mean_ssem.at[n], mean_rsem.at[n], to
            ))
    for copy in copies:
        copy.start()
    for copy in copies:
        copy.wait()
    sum1 = mean_send[0]
    for n in range(1, 8):
        sum1 = sum1 + mean_recv[n]
    mean_send[1] = sum1
    copies = [
        remote(
            mean_send.at[1], mean_recv.at[7 + d], mean_ssem.at[7 + d], mean_rsem.at[7 + d],
            place(a, g + d, z, c),
        )
        for d in (1, 2, 3)
    ]
    for copy in copies:
        copy.start()
    for copy in copies:
        copy.wait()
    sum2 = (mean_send[1] + mean_recv[9]) + (mean_recv[8] + mean_recv[10])
    mean_send[2] = sum2
    last = remote(
        mean_send.at[2], mean_recv.at[11], mean_ssem.at[11], mean_rsem.at[11],
        place(a, g, z + 2, c),
    )
    last.start()
    last.wait()
    everyone = jnp.sum(mean_send[2] + mean_recv[11], axis=-1, keepdims=True)
    o_mean[...] = jnp.broadcast_to(everyone / (32 * SEQ_ROWS), (8, 128))

    for copy in finals:
        copy.wait()
    theirs = pl.ds(pl.multiple_of(other * ROWS, ROWS), ROWS)
    o_trace[mine, :] = stat_mine[0]
    o_logp[mine, :] = stat_mine[1]
    o_trace[theirs, :] = stat_in[0]
    o_logp[theirs, :] = stat_in[1]


def per_device(
    latent, probe, time_embed, gain_attn, w_query, w_key, w_value, w_out, gain_mlp, w_in, w_down
):
    hbm = pl.BlockSpec(memory_space=pl.ANY)
    vmem = pl.BlockSpec(memory_space=pltpu.VMEM)
    dma = pltpu.SemaphoreType.DMA
    T = STEPS
    state, trace, logp, mean = pl.pallas_call(
        kernel,
        out_shape=(
            jax.ShapeDtypeStruct((SEQ_ROWS, WIDTH), f32),
            jax.ShapeDtypeStruct((SEQ_ROWS, 128), f32),
            jax.ShapeDtypeStruct((SEQ_ROWS, 128), f32),
            jax.ShapeDtypeStruct((8, 128), f32),
        ),
        in_specs=[hbm, hbm, vmem, vmem, hbm, hbm, hbm, hbm, vmem, hbm, hbm],
        out_specs=(vmem, vmem, vmem, vmem),
        scratch_shapes=[
            pltpu.VMEM((ROWS, WIDTH), bf16),
            pltpu.VMEM((ROWS, WIDTH), bf16),
            pltpu.VMEM((2, WIDTH, 256), bf16),
            pltpu.VMEM((2, WIDTH, 256), bf16),
            pltpu.VMEM((2, WIDTH, 256), bf16),
            pltpu.VMEM((2, 256, WIDTH), bf16),
            pltpu.VMEM((2, WIDTH, WIDTH), bf16),
            pltpu.VMEM((2, WIDTH, WIDTH), bf16),
            pltpu.VMEM((ROWS, WIDTH), f32),
            pltpu.VMEM((ROWS, WIDTH), f32),
            pltpu.VMEM((ROWS, WIDTH), f32),
            pltpu.VMEM((ROWS, 128), f32),
            pltpu.VMEM((2 * ROWS, WIDTH), f32),
            pltpu.VMEM((2 * ROWS, WIDTH), bf16),
            pltpu.VMEM((2, 2 * ROWS, WIDTH), bf16),
            pltpu.VMEM((T, 2, 4, ROWS, 256), bf16),
            pltpu.VMEM((T, 2, 4, ROWS, 128), bf16),
            pltpu.VMEM((T, 8, QROWS, 256), bf16),
            pltpu.VMEM((T, 8, ROWS, 128), bf16),
            pltpu.VMEM((QROWS, 128), bf16),
            pltpu.VMEM((QROWS, 128), bf16),
            pltpu.VMEM((T, QROWS, 256), bf16),
            pltpu.VMEM((QROWS, 128), f32),
            pltpu.VMEM((QROWS, 128), f32),
            pltpu.VMEM((QROWS, 128), f32),
            pltpu.VMEM((QROWS, 128), f32),
            pltpu.VMEM((QROWS, 128), f32),
            pltpu.VMEM((T, 8, ROWS, 128), bf16),
            pltpu.VMEM((T, 2, 4, ROWS, 128), bf16),
            pltpu.VMEM((T, 2, 2 * ROWS, WIDTH), bf16),
            pltpu.VMEM((T, 2, 2 * ROWS, WIDTH), bf16),
            pltpu.VMEM((2, ROWS, 128), f32),
            pltpu.VMEM((2, ROWS, 128), f32),
            pltpu.VMEM((3, 8, 128), f32),
            pltpu.VMEM((12, 8, 128), f32),
            dma((8,)),
            dma((6,)),
            dma((6,)),
            dma((T, 8)),
            dma((T, 8)),
            dma((T, 8)),
            dma((T, 8)),
            dma((3,)),
            dma((T, 32)),
            dma((T, 8, 4)),
            dma((T, 4)),
            dma((T, 8)),
            dma((T, 8)),
            dma((T, 2)),
            dma((T, 2)),
            dma((2,)),
            dma((2,)),
            dma((12,)),
            dma((12,)),
        ],
        compiler_params=pltpu.CompilerParams(
            collective_id=0, has_side_effects=True, vmem_limit_bytes=60 * 1024 * 1024
        ),
        name="flow",
    )(
        latent, probe, time_embed.reshape(1, WIDTH), gain_attn.reshape(1, WIDTH), w_query, w_key,
        w_value, w_out, gain_mlp.reshape(1, WIDTH), w_in, w_down,
    )
    return (state, trace[:, 0], logp[:, 0], mean[0, 0])


def solution(mesh):
    return jax.shard_map(
        per_device,
        mesh=mesh,
        in_specs=(
            P("seq", None),
            P("seq", None),
            P(),
            P(),
            P(None, "head"),
            P(None, "head"),
            P(None, "head"),
            P("head", None),
            P(),
            P(None, "head"),
            P("head", None),
        ),
        out_specs=(P("seq", None), P("seq"), P("seq"), P()),
        check_vma=False,
    )
```

time: 490 us -> 129 us (0.26)
  waiting for transfers between devices: 280 us -> 0 us
  Pallas kernels: 0 us -> 123 us
  blocking collectives: 121 us -> 0 us
  matrix products: 36.7 us -> 0 us
  other arithmetic: 23.1 us -> 0 us
  between operations: 16.4 us -> 0.64 us
  local copies, waits for them, and re-layouts: 12.3 us -> 4.56 us
    all_gather x2 -> x0, waiting for transfers between devices: 280 us -> none  [side_by_side(): filled, at, done = (lax.all_gather(both, axis, axis=dim, tiled=True), 0, [])]
    pallas_call x0 -> x1, Pallas kernels: none -> 123 us  [per_device(): pl.pallas_call(kernel, out_shape=(jax.ShapeDtypeStruct((SEQ_ROWS, WIDTH),...]
    all_to_all x5 -> x0, blocking collectives: 86.4 us -> none  [the longest x4 70.3 us: summed_on_arrival(): lax.all_to_all(tiles, axis, split_axis=0, concat_axis=0, tiled=True)]
    dot_general x24 -> x0, matrix products: 36.7 us -> none  [the longest x2 10.8 us: score_pair(): jnp.einsum('rhd,shd->hrs', queries, key_tang, preferred_element_type=jnp....]
    all_gather x5 -> x0, blocking collectives: 34.3 us -> none  [the longest x4 27.6 us: side_by_side(): filled, at, done = (lax.all_gather(both, axis, axis=dim, tiled=True), 0, [])]
    reduce_sum x14 -> x0, other arithmetic: 16.7 us -> none  [the longest x4 5.94 us: summed_on_arrival(): return arrived.sum(axis=0)]
    slice x17 -> x2, local copies, waits for them, and re-layouts: 10.9 us -> 2.67 us  [per_device(): return (state, trace[:, 0], logp[:, 0], mean[0, 0])]
  transfers between devices with their start and end apart: 2 -> 0, of which waited for: 2 -> 0; matrix products, arithmetic and copies ran while one was open for 1% -> 0% of each run, Pallas kernels for 0% -> 0%
where the time goes in v1:
time: 129 us
  Pallas kernels  123 us (95%)
  local copies, waits for them, and re-layouts  4.56 us (4%)
    pallas_call x1, Pallas kernels, per_device(): pl.pallas_call(kernel, out_shape=(jax.ShapeDtypeStruct((SEQ_ROWS, WIDTH),...  123 us
    slice x2, local copies, waits for them, and re-layouts, per_device(): return (state, trace[:, 0], logp[:, 0], mean[0, 0])  2.67 us

profile of v1, /device:TPU:0, one launch (start us, length us, event | category | flops | bytes accessed | tf_op | source)
XLA Modules:
  0.0 128.6 jit_solution(9532110291181774947)
XLA Ops:
  0.6 123.4 %flow.1 = (f32[128,1024]{1,0:T(8,128)}, f32[128,128]{1,0:T(8,128)}, f32[128,128]{1,0:T(8,128)}, f32[8,128]{1,0:T(8,128)}) custom-call(bf16[128,1024]{1,0:T(8,128)(2,1)} %latent.1, bf16[128,1024]{1,0:T(8,128)(2,1)} %probe.1, f32[1,1024]{1,0:T(1,128)} %bitcast.4, f32[1,1024]{1,0:T(1,128)} %bitcast.5, bf16[1024,256]{1,0:T(8,128)(2,1)} %w_query.1, ...), custom_call_target="tpu_custom_call" | custom-call | tf_op jit(solution)/shard_map/flow/pallas_call | solution.py:510
  124.0 1.5 %slice_reduce_fusion = (f32[128]{0:T(128)}, f32[128]{0:T(128)}) fusion(f32[128,128]{1,0:T(8,128)} %get-tuple-element.10, f32[128,128]{1,0:T(8,128)} %get-tuple-element.9), kind=kLoop, calls=%fused_computation | loop fusion | bytes 2048 | tf_op jit(solution)/shard_map/slice | solution.py:584
  125.5 1.2 slice.11
  126.7 1.9 %copy.16 = f32[128,1024]{1,0:T(8,128)} copy(f32[128,1024]{1,0:T(8,128)} %get-tuple-element.18) | data formatting | bytes 1048576

commit v2 on v1

v2 whole, which is shorter than its diff:
```python
import functools
import math

import jax
import jax.numpy as jnp
from jax import lax
from jax.experimental import pallas as pl
from jax.experimental.pallas import tpu as pltpu
from jax.sharding import PartitionSpec as P

HEAD_DIM = 64
STEPS = 2
EPSILON = 1e-05
GELU_COEF = 0.044715
ROOT_TWO_PI = math.sqrt(2.0 / math.pi)

ROWS = 64
SEQ_ROWS = 128
WIDTH = 1024
RING = 4
QROWS = 512
NEG = -1e30

CHUNK = 256

OWN, LEFT, RIGHT, FAR, ZOWN, ZLEFT, ZRIGHT, ZFAR = range(8)

f32 = jnp.float32
bf16 = jnp.bfloat16


def norm_pair(values, tangent, norm_gain):
    meansq = jnp.mean(values * values, axis=-1, keepdims=True) + EPSILON
    inverse = lax.rsqrt(meansq)
    inner_mean = jnp.mean(values * tangent, axis=-1, keepdims=True)
    primal = values * inverse * norm_gain
    derived = (tangent * inverse - values * inverse**3 * inner_mean) * norm_gain
    return jnp.concatenate([primal.astype(bf16), derived.astype(bf16)], axis=0)


def gelu_pair(pre_act, tangent):
    cubic_arg = pre_act + GELU_COEF * pre_act * pre_act * pre_act
    tanh_value = jnp.tanh(ROOT_TWO_PI * cubic_arg)
    output = 0.5 * pre_act * (1.0 + tanh_value)
    slope_value = 0.5 * (1.0 + tanh_value) + 0.5 * pre_act * (
        1.0 - tanh_value * tanh_value
    ) * ROOT_TWO_PI * (1.0 + 3.0 * GELU_COEF * pre_act * pre_act)
    return (output.astype(bf16), (slope_value * tangent).astype(bf16))


def swap_halves(tile):
    return pltpu.roll(tile, HEAD_DIM, 1)


def kernel(
    latent, probe, time_embed, gain_attn, w_query, w_key, w_value, w_out, gain_mlp, w_in, w_down,
    o_state, o_stats,
    lat_in, prb_in, wq, wk, wv, wo, wi, wd,
    state, direction, inputs_s, trace_s, attn_s, normed_s, act_s, probe_down,
    stage_kv, stage_q, kv, qin, q1, q2, acc_p, acc_t, top_s, total_s, carried_s,
    ret_stage, ret, red_send, red_recv, part_send, part_recv, stat_mine, stat_in,
    mean_send, mean_recv,
    load_sem, wsend, wrecv, out_send, out_recv, kv_send, kv_recv, q_send, q_recv, self_sem,
    g_send, g_recv, ret_send, ret_recv, red_ssem, red_rsem, fin_send, fin_recv,
    mean_ssem, mean_rsem,
):
    s = lax.axis_index("seq")
    hd = lax.axis_index("head")
    x = lax.rem(s // 4, 4)
    y = lax.rem(s, 4)
    c = lax.rem(hd, 2)
    other = 1 - c
    zlo = hd // 2
    z = (s // 16) * 2 + zlo
    a = y + c * (x - y)
    g = x + c * (y - x)

    def place(aa, gg, zz, cc):
        aa, gg, zz = lax.rem(aa, 4), lax.rem(gg, 4), lax.rem(zz, 4)
        xx = gg + c * (aa - gg)
        yy = aa + c * (gg - aa)
        return ((zz // 2) * 16 + xx * 4 + yy, lax.rem(zz, 2) * 2 + cc)

    def remote(src, dst, ssem, rsem, where):
        return pltpu.make_async_remote_copy(
            src_ref=src, dst_ref=dst, send_sem=ssem, recv_sem=rsem,
            device_id=where, device_id_type=pl.DeviceIdType.MESH,
        )

    here = place(a, g, z, other)
    zpair = z + 1 - 2 * zlo
    znext = z + 3 + 2 * zlo
    zfar = z + 2

    def both_ways(zz, first):
        return (
            [place(a + d, g, zz, c) for d in range(first, 4)]
            + [place(a + d, g, zz, other) for d in range(4)]
            + [place(a, g + d, zz, other) for d in (1, 2, 3)]
        )

    barrier = pltpu.get_barrier_semaphore()
    greeted = (
        both_ways(z, 1) + both_ways(zfar, 0) + both_ways(zpair, 0)
        + [place(a, g + d, z, c) for d in (1, 2, 3)]
        + [place(a, g + d, znext, c) for d in range(4)]
    )
    for where in greeted:
        pl.semaphore_signal(
            barrier, inc=1, device_id=where, device_id_type=pl.DeviceIdType.MESH
        )

    row0 = pl.multiple_of(c * ROWS, ROWS)
    loads = [
        pltpu.make_async_copy(latent.at[pl.ds(row0, ROWS)], lat_in, load_sem.at[0]),
        pltpu.make_async_copy(probe.at[pl.ds(row0, ROWS)], prb_in, load_sem.at[1]),
    ]
    weights = [(w_key, wk), (w_value, wv), (w_query, wq), (w_in, wi), (w_down, wd)]
    for i, (src, dst) in enumerate(weights):
        loads.append(pltpu.make_async_copy(src, dst.at[c], load_sem.at[2 + i]))
    loads.append(pltpu.make_async_copy(w_out, wo.at[hd], load_sem.at[7]))
    for load in loads:
        load.start()
    pl.semaphore_wait(barrier, len(greeted))
    swaps = [
        remote(src, dst.at[c], wsend.at[i], wrecv.at[i], here)
        for i, (src, dst) in enumerate(weights)
    ]
    out_here = remote(w_out, wo.at[hd], out_send.at[0], out_recv.at[0], here)
    out_pair = remote(
        w_out, wo.at[hd], out_send.at[1], out_recv.at[1], place(a, g, zpair, c)
    )
    pair_hd = 2 * (1 - zlo) + c
    out_on = remote(wo.at[pair_hd], wo.at[pair_hd], out_send.at[2], out_recv.at[2], here)
    for swap in swaps[:3] + [out_pair, out_here] + swaps[3:]:
        swap.start()

    loads[0].wait()
    loads[1].wait()
    state[...] = lat_in[...].astype(f32)
    direction[...] = prb_in[...].astype(f32)
    trace_s[...] = jnp.zeros_like(trace_s)

    lane = lax.broadcasted_iota(jnp.int32, (ROWS, 128), 1)
    low = lane < HEAD_DIM
    low_c = lax.broadcasted_iota(jnp.int32, (128, 128), 1) < HEAD_DIM
    low_t = lax.broadcasted_iota(jnp.int32, (8, 128), 1) < ROWS

    def weights_here(first, last):
        for i in range(first, last):
            loads[2 + i].wait()
            swaps[i].wait()

    def rows_to_lanes(first, second):
        tall = jnp.concatenate(
            [jnp.broadcast_to(first, (ROWS, 128)), jnp.broadcast_to(second, (ROWS, 128))], axis=0
        )
        return jnp.transpose(tall)[:8]

    def one_step(t, carry):
        inputs = state[...] + (t.astype(f32) / STEPS) * time_embed[...]
        inputs_s[...] = inputs
        normed_s[...] = norm_pair(inputs, direction[...], gain_attn[...])
        normed = normed_s[...]

        @pl.when(t == 0)
        def _():
            weights_here(0, 2)

        def project(weight, fill, scale):
            for cc in range(2):
                both = jnp.dot(normed, weight[cc], preferred_element_type=f32)
                if scale is not None:
                    both = both * scale
                for j in range(2):
                    prim = both[:ROWS, j * 128 : (j + 1) * 128]
                    tang = both[ROWS:, j * 128 : (j + 1) * 128]
                    fill(cc, 2 * j, jnp.where(low, prim, swap_halves(tang)).astype(bf16))
                    fill(cc, 2 * j + 1, jnp.where(low, swap_halves(prim), tang).astype(bf16))

        def kv_slot(block, slot, kind):
            return kv.at[t, block, pl.ds((slot * 2 + kind) * ROWS, ROWS)]

        def q_slot(slot, kind):
            return qin.at[t, slot * 2 + kind]

        def fill_key(cc, head, value):
            stage_kv[t, cc, head, :, :128] = value

        def fill_val(cc, head, value):
            stage_kv[t, cc, head, :, 128:] = value

        def fill_query(cc, head, value):
            stage_q[t, cc, head] = value

        project(wk, fill_key, None)
        project(wv, fill_val, None)

        kv_out, q_out = [], []
        for d in (2, 1, 3, 0):
            slot = (4 - d) % 4
            for kind in (1, 0):
                n = slot * 2 + kind
                if kind == 0:
                    cc, head = c, lax.rem(a + d, 4)
                else:
                    cc, head = other, lax.rem(g + d, 4)
                for block, zz, row in ((ZOWN, zfar, 1), (OWN, z, 0)):
                    to = place(a + d, g, zz, c) if kind == 0 else place(a, g + d, zz, other)
                    if n == 0 and block == OWN:
                        continue
                    copy = remote(
                        stage_kv.at[t, cc, head], kv_slot(block, slot, kind),
                        kv_send.at[t, row, n], kv_recv.at[t, row, n], to,
                    )
                    copy.start()
                    kv_out.append(copy)
        kv_self = pltpu.make_async_copy(stage_kv.at[t, c, a], kv_slot(OWN, 0, 0), self_sem.at[0])
        kv_self.start()

        @pl.when(t == 0)
        def _():
            weights_here(2, 3)

        project(wq, fill_query, HEAD_DIM**-0.5)
        for d in (2, 1, 3, 0):
            slot = (4 - d) % 4
            for kind in (1, 0):
                n = slot * 2 + kind
                if n == 0:
                    continue
                if kind == 0:
                    cc, head, to = c, lax.rem(a + d, 4), place(a + d, g, z, c)
                else:
                    cc, head, to = other, lax.rem(g + d, 4), place(a, g + d, z, other)
                copy = remote(
                    stage_q.at[t, cc, head], q_slot(slot, kind), q_send.at[t, n],
                    q_recv.at[t, n], to,
                )
                copy.start()
                q_out.append(copy)
        q_self = pltpu.make_async_copy(stage_q.at[t, c, a], q_slot(0, 0), self_sem.at[1])
        q_self.start()

        def piece(block, p):
            return kv.at[t, block, pl.ds(p * 128, 128)]

        sent = []

        def send(src, block, p, to):
            n = len(sent)
            copy = remote(src, piece(block, p), g_send.at[t, n], g_recv.at[t, block, p], to)
            copy.start()
            sent.append(copy)

        right, left = place(a, g + 1, z, c), place(a, g + 3, z, c)
        across = place(a, g + 2, z, c)

        def arrived(block, p):
            remote(
                piece(block, p), piece(block, p), g_send.at[t, 0], g_recv.at[t, block, p], right
            ).wait_recv()

        def slot_here(block, slot, row):
            for kind in range(2):
                n = slot * 2 + kind
                if n == 0 and block == OWN:
                    kv_self.wait()
                else:
                    part = kv_slot(block, slot, kind)
                    remote(
                        part, part, kv_send.at[t, row, n], kv_recv.at[t, row, n], right
                    ).wait_recv()

        for slot in (0, 1, 3, 2):
            slot_here(OWN, slot, 0)
            send(piece(OWN, slot), LEFT, slot, right)
            send(piece(OWN, slot), RIGHT, slot, left)

        def spread(slot):
            slot_here(ZOWN, slot, 1)
            send(piece(ZOWN, slot), ZFAR, slot, across)
            send(piece(ZOWN, slot), ZLEFT, slot, right)
            send(piece(ZOWN, slot), ZRIGHT, slot, left)

        for n in range(8):
            if n == 0:
                q_self.wait()
            else:
                remote(
                    qin.at[t, n], qin.at[t, n], q_send.at[t, n], q_recv.at[t, n], right
                ).wait_recv()

        def prepare(n, carry):
            tile = qin[t, n].astype(f32)
            q1[pl.ds(n * ROWS, ROWS), :] = jnp.where(low, tile, 0.0).astype(bf16)
            q2[pl.ds(n * ROWS, ROWS), :] = swap_halves(tile).astype(bf16)
            return carry

        lax.fori_loop(0, 8, prepare, 0)
        acc_p[...] = jnp.zeros_like(acc_p)
        acc_t[...] = jnp.zeros_like(acc_t)
        total_s[...] = jnp.zeros_like(total_s)
        carried_s[...] = jnp.zeros_like(carried_s)
        top_s[...] = jnp.full_like(top_s, NEG)

        def attend(block):
            keys = kv[t, block, :, 0:128]
            vals = kv[t, block, :, 128:256]
            nt = (((1,), (1,)), ((), ()))

            def chunk(i, carry):
                at = pl.ds(pl.multiple_of(i * CHUNK, CHUNK), CHUNK)
                both = lax.dot_general(
                    jnp.concatenate([q1[at, :], q2[at, :]], axis=0), keys, nt,
                    preferred_element_type=f32,
                )
                scores, tangs = both[:CHUNK], both[CHUNK:]
                old = top_s[at, :]
                new = jnp.maximum(old, jnp.max(scores, axis=-1, keepdims=True))
                fade = jnp.exp(old - new)
                top_s[at, :] = new
                weights_ = jnp.exp(scores - jnp.concatenate([new] * 4, axis=1))
                weighted = weights_ * tangs
                tot = fade * total_s[at, :]
                car = fade * carried_s[at, :]
                for k in range(4):
                    tot = tot + weights_[:, k * 128 : (k + 1) * 128]
                    car = car + weighted[:, k * 128 : (k + 1) * 128]
                total_s[at, :] = tot
                carried_s[at, :] = car
                out = jnp.dot(
                    jnp.concatenate([weights_.astype(bf16), weighted.astype(bf16)], axis=0), vals,
                    preferred_element_type=f32,
                )
                acc_p[at, :] = fade * acc_p[at, :] + out[:CHUNK]
                acc_t[at, :] = fade * acc_t[at, :] + out[CHUNK:]
                return carry

            lax.fori_loop(0, QROWS // CHUNK, chunk, 0, unroll=True)

        attend(OWN)
        spread(0)
        spread(1)
        for p in (0, 1):
            arrived(LEFT, p)
            send(piece(LEFT, p), FAR, p, right)
        for p in (3, 2):
            arrived(RIGHT, p)
            send(piece(RIGHT, p), FAR, p, left)
        arrived(LEFT, 3)
        arrived(LEFT, 2)
        attend(LEFT)
        spread(3)
        spread(2)
        arrived(RIGHT, 0)
        arrived(RIGHT, 1)
        attend(RIGHT)

        @pl.when(t == 0)
        def _():
            weights_here(3, 5)
            for cc in range(2):
                def down(j, carry):
                    at = pl.ds(pl.multiple_of(j * 256, 256), 256)
                    probe_down[cc, :, at] = lax.dot_general(
                        prb_in[...], wd[cc, at, :], (((1,), (1,)), ((), ())),
                        preferred_element_type=f32,
                    )
                    return carry

                lax.fori_loop(0, 4, down, 0)

        attend(ZOWN)
        for p in range(4):
            arrived(FAR, p)
        attend(FAR)

        @pl.when(t == 0)
        def _():
            loads[7].wait()
            out_pair.wait_recv()
            out_on.start()

        for block in (ZLEFT, ZRIGHT, ZFAR):
            for p in (0, 1, 3, 2):
                arrived(block, p)
            attend(block)

        def finish(i, carry):
            at = pl.ds(pl.multiple_of(i * 128, 128), 128)
            total = jnp.sum(total_s[at, :], axis=-1, keepdims=True)
            carried = jnp.sum(carried_s[at, :], axis=-1, keepdims=True)
            ap = acc_p[at, :]
            prim = ap / total
            tang = (acc_t[at, :] + swap_halves(ap)) / total - (carried / total) * prim
            out = jnp.where(low_c, prim, swap_halves(tang)).astype(bf16)
            ret_stage[t, 2 * i] = out[:ROWS]
            ret_stage[t, 2 * i + 1] = out[ROWS:]
            return carry

        lax.fori_loop(0, 4, finish, 0)

        back = []
        for slot in (2, 1, 3, 0):
            for kind in (0, 1):
                n = slot * 2 + kind
                m = ((4 - slot) % 4) * 2 + kind
                for row, zz in ((1, zpair), (0, z)):
                    if n == 0 and row == 0:
                        continue
                    copy = remote(
                        ret_stage.at[t, n], ret.at[t, hd, a], ret_send.at[t, row, n],
                        ret_recv.at[t, row, m], place(a + slot, g, zz, c if kind == 0 else other),
                    )
                    copy.start()
                    back.append(copy)
        ret_self = pltpu.make_async_copy(ret_stage.at[t, 0], ret.at[t, hd, a], self_sem.at[2])
        ret_self.start()

        @pl.when(t == 0)
        def _():
            out_here.wait()
            out_pair.wait_send()
            out_on.wait()

        ret_self.wait()
        for row in range(2):
            for m in range(8):
                if m == 0 and row == 0:
                    continue
                remote(
                    ret_stage.at[t, 0], ret.at[t, 0, 0], ret_send.at[t, row, m],
                    ret_recv.at[t, row, m], right,
                ).wait_recv()

        prims, tangs = [], []
        for cc in range(4):
            for j in range(2):
                first = ret[t, cc, 2 * j].astype(f32)
                second = ret[t, cc, 2 * j + 1].astype(f32)
                prims.append(jnp.where(low, first, swap_halves(second)).astype(bf16))
                tangs.append(jnp.where(low, swap_halves(first), second).astype(bf16))
        part = jnp.zeros((2 * ROWS, WIDTH), f32)
        for cc in range(4):
            heads = jnp.concatenate(
                [
                    jnp.concatenate(prims[2 * cc : 2 * cc + 2], axis=1),
                    jnp.concatenate(tangs[2 * cc : 2 * cc + 2], axis=1),
                ],
                axis=0,
            )
            part = part + jnp.dot(heads, wo[cc], preferred_element_type=f32)
        attn_s[...] = part
        middle = inputs_s[...] + attn_s[:ROWS, :]
        middle_tang = direction[...] + attn_s[ROWS:, :]
        normed_s[...] = norm_pair(middle, middle_tang, gain_mlp[...])

        normed2 = normed_s[...]
        part_s = jnp.zeros((ROWS, 256), f32)
        for cc in range(2):
            for j in range(4):
                at = slice(j * 256, (j + 1) * 256)
                pre = jnp.dot(normed2, wi[cc, :, at], preferred_element_type=f32)
                act, act_tang = gelu_pair(pre[:ROWS], pre[ROWS:])
                act_s[cc, :, at] = act
                part_s = part_s + act_tang.astype(f32) * probe_down[cc, :, at]
        pair = place(a, g, zpair, c)
        sums = []
        for j in range(4):
            at = slice(j * 256, (j + 1) * 256)
            red_send[t, j] = (
                jnp.dot(act_s[0], wd[0, :, at], preferred_element_type=f32)
                + jnp.dot(act_s[1], wd[1, :, at], preferred_element_type=f32)
            ).astype(bf16)
            copy = remote(
                red_send.at[t, j], red_recv.at[t, j], red_ssem.at[t, j], red_rsem.at[t, j], pair
            )
            copy.start()
            sums.append(copy)
        part_send[t] = rows_to_lanes(
            jnp.sum(part_s, axis=-1, keepdims=True),
            jnp.sum(direction[...] * attn_s[ROWS:, :], axis=-1, keepdims=True),
        )
        copy = remote(
            part_send.at[t], part_recv.at[t], red_ssem.at[t, 4], red_rsem.at[t, 4], pair
        )
        copy.start()
        for j, summed in enumerate(sums):
            at = slice(j * 256, (j + 1) * 256)
            summed.wait()
            mlp = red_send[t, j].astype(f32) + red_recv[t, j].astype(f32)
            state[:, at] = state[:, at] + (attn_s[:ROWS, at] + mlp) / STEPS
        copy.wait()
        share = part_send[t]
        trace_s[...] = trace_s[...] + (
            (share + part_recv[t]) + pltpu.roll(share, ROWS, 1)
        ) / (STEPS * WIDTH)

        for copy in kv_out + q_out + sent + back:
            copy.wait_send()
        return carry

    lax.fori_loop(0, STEPS, one_step, 0)

    final = state[...]
    squares = jnp.sum(final * final, axis=-1, keepdims=True)
    trace = trace_s[...]
    logp = (
        trace - 0.5 * rows_to_lanes(squares, squares) / WIDTH - 0.5 * math.log(2.0 * math.pi)
    )
    trace = jnp.where(low_t, trace, 0.0)
    logp = jnp.where(low_t, logp, 0.0)
    first = c == 0
    stat_mine[0] = jnp.where(first, trace, pltpu.roll(trace, ROWS, 1))
    stat_mine[1] = jnp.where(first, logp, pltpu.roll(logp, ROWS, 1))
    spot = lax.broadcasted_iota(jnp.int32, (8, 128), 1) == s * 2 + c
    mean_send[0] = jnp.where(spot, jnp.sum(logp, axis=-1, keepdims=True), 0.0)
    mine = pl.ds(row0, ROWS)
    finals = [
        remote(state, o_state.at[mine], fin_send.at[0], fin_recv.at[0], here),
        remote(stat_mine, stat_in, fin_send.at[1], fin_recv.at[1], here),
    ]
    for copy in finals:
        copy.start()
    o_state[mine, :] = final

    copies = []
    for d in range(4):
        slot = (4 - d) % 4
        for kind in range(2):
            if kind == 0 and d == 0:
                continue
            to = place(a + d, g, z, c) if kind == 0 else place(a, g + d, z, other)
            n = slot * 2 + kind
            copies.append(remote(
                mean_send.at[0], mean_recv.at[n], mean_ssem.at[n], mean_rsem.at[n], to
            ))
    for copy in copies:
        copy.start()
    for copy in copies:
        copy.wait()
    sum1 = mean_send[0]
    for n in range(1, 8):
        sum1 = sum1 + mean_recv[n]
    mean_send[1] = sum1
    copies = []
    for row, zz in ((1, znext), (0, z)):
        for d in (2, 1, 3, 0):
            if d == 0 and row == 0:
                continue
            n = 8 + row * 4 + d
            copies.append(remote(
                mean_send.at[1], mean_recv.at[n], mean_ssem.at[n], mean_rsem.at[n],
                place(a, g + d, zz, c),
            ))
    for copy in copies:
        copy.start()
    for copy in copies:
        copy.wait()
    everyone = mean_send[1]
    for n in range(9, 16):
        everyone = everyone + mean_recv[n]
    everyone = jnp.sum(everyone, axis=-1, keepdims=True)
    o_stats[2] = jnp.broadcast_to(everyone / (32 * SEQ_ROWS), (8, 128))
    for copy in finals:
        copy.wait()
    o_stats[0] = stat_mine[0] + stat_in[0]
    o_stats[1] = stat_mine[1] + stat_in[1]


def write_out(state, stats, o_state, o_trace, o_logp, o_mean):
    o_state[...] = state[...]
    o_trace[...] = stats[0, 0:1, :]
    o_logp[...] = stats[1, 0:1, :]
    o_mean[...] = stats[2, 0:1, 0:1]


def per_device(
    latent, probe, time_embed, gain_attn, w_query, w_key, w_value, w_out, gain_mlp, w_in, w_down
):
    hbm = pl.BlockSpec(memory_space=pl.ANY)
    vmem = pl.BlockSpec(memory_space=pltpu.VMEM)
    dma = pltpu.SemaphoreType.DMA
    T = STEPS
    state, stats = pl.pallas_call(
        kernel,
        out_shape=(
            jax.ShapeDtypeStruct((SEQ_ROWS, WIDTH), f32),
            jax.ShapeDtypeStruct((3, 8, 128), f32),
        ),
        in_specs=[hbm, hbm, vmem, vmem, hbm, hbm, hbm, hbm, vmem, hbm, hbm],
        out_specs=(vmem, vmem),
        scratch_shapes=[
            pltpu.VMEM((ROWS, WIDTH), bf16),
            pltpu.VMEM((ROWS, WIDTH), bf16),
            pltpu.VMEM((2, WIDTH, 256), bf16),
            pltpu.VMEM((2, WIDTH, 256), bf16),
            pltpu.VMEM((2, WIDTH, 256), bf16),
            pltpu.VMEM((4, 256, WIDTH), bf16),
            pltpu.VMEM((2, WIDTH, WIDTH), bf16),
            pltpu.VMEM((2, WIDTH, WIDTH), bf16),
            pltpu.VMEM((ROWS, WIDTH), f32),
            pltpu.VMEM((ROWS, WIDTH), f32),
            pltpu.VMEM((ROWS, WIDTH), f32),
            pltpu.VMEM((8, 128), f32),
            pltpu.VMEM((2 * ROWS, WIDTH), f32),
            pltpu.VMEM((2 * ROWS, WIDTH), bf16),
            pltpu.VMEM((2, ROWS, WIDTH), bf16),
            pltpu.VMEM((2, ROWS, WIDTH), f32),
            pltpu.VMEM((T, 2, 4, ROWS, 256), bf16),
            pltpu.VMEM((T, 2, 4, ROWS, 128), bf16),
            pltpu.VMEM((T, 8, QROWS, 256), bf16),
            pltpu.VMEM((T, 8, ROWS, 128), bf16),
            pltpu.VMEM((QROWS, 128), bf16),
            pltpu.VMEM((QROWS, 128), bf16),
            pltpu.VMEM((QROWS, 128), f32),
            pltpu.VMEM((QROWS, 128), f32),
            pltpu.VMEM((QROWS, 128), f32),
            pltpu.VMEM((QROWS, 128), f32),
            pltpu.VMEM((QROWS, 128), f32),
            pltpu.VMEM((T, 8, ROWS, 128), bf16),
            pltpu.VMEM((T, 4, 4, ROWS, 128), bf16),
            pltpu.VMEM((T, 4, ROWS, 256), bf16),
            pltpu.VMEM((T, 4, ROWS, 256), bf16),
            pltpu.VMEM((T, 8, 128), f32),
            pltpu.VMEM((T, 8, 128), f32),
            pltpu.VMEM((2, 8, 128), f32),
            pltpu.VMEM((2, 8, 128), f32),
            pltpu.VMEM((2, 8, 128), f32),
            pltpu.VMEM((16, 8, 128), f32),
            dma((8,)),
            dma((5,)),
            dma((5,)),
            dma((3,)),
            dma((3,)),
            dma((T, 2, 8)),
            dma((T, 2, 8)),
            dma((T, 8)),
            dma((T, 8)),
            dma((3,)),
            dma((T, 24)),
            dma((T, 8, 4)),
            dma((T, 2, 8)),
            dma((T, 2, 8)),
            dma((T, 5)),
            dma((T, 5)),
            dma((2,)),
            dma((2,)),
            dma((16,)),
            dma((16,)),
        ],
        compiler_params=pltpu.CompilerParams(
            collective_id=0, has_side_effects=True, vmem_limit_bytes=60 * 1024 * 1024
        ),
        name="flow",
    )(
        latent, probe, time_embed.reshape(1, WIDTH), gain_attn.reshape(1, WIDTH), w_query, w_key,
        w_value, w_out, gain_mlp.reshape(1, WIDTH), w_in, w_down,
    )
    state, trace, logp, mean = pl.pallas_call(
        write_out,
        out_shape=(
            jax.ShapeDtypeStruct((SEQ_ROWS, WIDTH), f32),
            jax.ShapeDtypeStruct((1, SEQ_ROWS), f32),
            jax.ShapeDtypeStruct((1, SEQ_ROWS), f32),
            jax.ShapeDtypeStruct((1, 1), f32),
        ),
        in_specs=[vmem, vmem],
        out_specs=(vmem, vmem, vmem, vmem),
        name="write_out",
    )(state, stats)
    return (state, trace.reshape(SEQ_ROWS), logp.reshape(SEQ_ROWS), mean.reshape(()))


def solution(mesh):
    return jax.shard_map(
        per_device,
        mesh=mesh,
        in_specs=(
            P("seq", None),
            P("seq", None),
            P(),
            P(),
            P(None, "head"),
            P(None, "head"),
            P(None, "head"),
            P("head", None),
            P(),
            P(None, "head"),
            P("head", None),
        ),
        out_specs=(P("seq", None), P("seq"), P("seq"), P()),
        check_vma=False,
    )
```

time: 129 us -> 102 us (0.79)
  Pallas kernels: 123 us -> 101 us
  local copies, waits for them, and re-layouts: 4.56 us -> 0 us
    pallas_call x1, Pallas kernels: 123 us -> 98.9 us  [per_device(): pl.pallas_call(kernel, out_shape=(jax.ShapeDtypeStruct((SEQ_ROWS, WIDTH),...]
    slice x2 -> x0, local copies, waits for them, and re-layouts: 2.67 us -> none  [per_device(): return (state, trace[:, 0], logp[:, 0], mean[0, 0])]
    unnamed x1 -> x0, local copies, waits for them, and re-layouts: 1.88 us -> none
    pallas_call x0 -> x1, Pallas kernels: none -> 1.88 us  [per_device(): pl.pallas_call(write_out, out_shape=(jax.ShapeDtypeStruct((SEQ_ROWS, WIDT...]
where the time goes in v2:
time: 102 us; the launch traced here: 101 us
  Pallas kernels  101 us (99%)
    pallas_call x1, Pallas kernels, per_device(): pl.pallas_call(kernel, out_shape=(jax.ShapeDtypeStruct((SEQ_ROWS, WIDTH),...  98.9 us

profile of v2, /device:TPU:0, one launch (start us, length us, event | category | flops | bytes accessed | tf_op | source)
XLA Modules:
  0.0 101.4 jit_solution(7815186296972882958)
XLA Ops:
  0.6 98.9 %flow.1 = (f32[128,1024]{1,0:T(8,128)}, f32[3,8,128]{2,1,0:T(8,128)}) custom-call(bf16[128,1024]{1,0:T(8,128)(2,1)} %latent.1, bf16[128,1024]{1,0:T(8,128)(2,1)} %probe.1, f32[1,1024]{1,0:T(1,128)} %bitcast.6, f32[1,1024]{1,0:T(1,128)} %bitcast.7, bf16[1024,256]{1,0:T(8,128)(2,1)} %w_query.1, bf16[1024,256]{1,0:T(8,128)(2,1)} %w_key.1, ...), custom_call_target="tpu_custom_call" | custom-call | tf_op jit(solution)/shard_map/flow/pallas_call | solution.py:586
  99.5 1.9 %write_out.1 = (f32[128,1024]{1,0:T(8,128)}, f32[1,128]{1,0:T(1,128)}, f32[1,128]{1,0:T(1,128)}, f32[1,1]{1,0:T(1,128)}) custom-call(f32[128,1024]{1,0:T(8,128)} %get-tuple-element.10.state, f32[3,8,128]{2,1,0:T(8,128)} %get-tuple-element.11.stats), custom_call_target="tpu_custom_call" | custom-call | tf_op jit(solution)/shard_map/write_out/pallas_call | solution.py:661
